TPU v7x, 32 devices: a whole 2x2x4 slice. The times are simulated.
32 devices in a mesh: path: 8 (over y, x, core), mod: 4 (over z).
Axes of the slice: x: 2, y: 2, z: 4, core: 2. Of those that a mesh axis runs over, the one named last changes fastest.
Arguments:
- activations: bfloat16 [8, 512, 4096], P('path', 'mod'), may hold values from -6 to 6
- cotangent: bfloat16 [8, 512, 4096], P('path', 'mod'), may hold values from -6 to 6
- first_weight: bfloat16 [8, 4096, 4096], P('path', None, 'mod'), may hold values from -6 to 6
- second_weight: bfloat16 [8, 4096, 4096], P('path', None, 'mod'), may hold values from -6 to 6
- first_master: float32 [4, 4096, 4096], P(None, ('path', 'mod')), may hold values from -6 to 6
- second_master: float32 [4, 4096, 4096], P(None, ('path', 'mod')), may hold values from -6 to 6
- first_moment: float32 [4, 4096, 4096], P(None, ('path', 'mod')), may hold values from -3 to 3
- second_moment: float32 [4, 4096, 4096], P(None, ('path', 'mod')), may hold values from -3 to 3
- routing: int32 [8, 2], replicated, may hold values from 0 to 3, as said below
Outputs:
- first_result: bfloat16 [8, 4096, 4096], P('path', None, 'mod')
- second_result: bfloat16 [8, 4096, 4096], P('path', None, 'mod')
Inputs may be any that keep to these rules, and one draw needn't show every extreme that they name: `routing`: for each of the two levels, every one of the 4 modules is taken by at least one path.
All inputs are finite; a program needn't handle non-finite values.
Results may differ from a plain program's by a relative error of at most 0.0045.
Values may be sent and summed in bfloat16 or wider, within the bound.
A program may use at most 192 MiB of HBM per device.

v0:
```python
import functools

import jax
import jax.numpy as jnp
from jax import lax
from jax.experimental import pallas as pl
from jax.experimental.pallas import tpu as pltpu
from jax.sharding import PartitionSpec as P

inner_rate = 1.0
outer_rate = 0.7
momentum_decay = 0.9

mean_factor = outer_rate * (1.0 + momentum_decay)
master_factor = 1.0 - mean_factor
moment_factor = -outer_rate * momentum_decay * momentum_decay

ANY = pl.BlockSpec(memory_space=pl.ANY)


def remote(src, dst, send_sem, recv_sem, where):
    return pltpu.make_async_remote_copy(
        src_ref=src,
        dst_ref=dst,
        send_sem=send_sem,
        recv_sem=recv_sem,
        device_id=where,
        device_id_type=pl.DeviceIdType.MESH,
    )


def run_all(copies):
    for copy in copies:
        copy.start()
    for copy in copies:
        copy.wait()


def scatter_kernel(
    paths, groups, t0, t1, b0, b1, a0, a1, c0, c1, send, recv, zsend, zrecv, local
):
    p = lax.axis_index("path")
    z = lax.axis_index("mod")
    rows = a0.shape[1]
    owned = b0.shape[1]
    columns = a0.shape[2]
    copies = []
    locals_ = []
    for level, (t, a) in enumerate(((t0, a0), (t1, a1))):
        own = t.at[pl.ds(p * rows, rows), :]
        locals_.append(pltpu.make_async_copy(own, a.at[p], local.at[level]))
    for level, (b, c) in enumerate(((b0, c0), (b1, c1))):
        own = b.at[:, :, pl.ds(pl.multiple_of(z * columns, columns), columns)]
        locals_.append(
            pltpu.make_async_copy(own, c.at[:, pl.ds(z * owned, owned), :], local.at[2 + level])
        )
    for level, (b, c) in enumerate(((b0, c0), (b1, c1))):
        for step in range(1, groups):
            to = lax.rem(z + step, groups)
            copies.append(
                remote(
                    b.at[:, :, pl.ds(pl.multiple_of(to * columns, columns), columns)],
                    c.at[:, pl.ds(z * owned, owned), :],
                    zsend.at[level, step],
                    zrecv.at[level, step],
                    (p, to),
                )
            )
    order = []
    for level, (t, a) in enumerate(((t0, a0), (t1, a1))):
        for step in range(paths - 1, 0, -1):
            to = lax.rem(p + step, paths)
            order.append(
                remote(
                    t.at[pl.ds(to * rows, rows), :],
                    a.at[p],
                    send.at[level, step],
                    recv.at[level, step],
                    (to, z),
                )
            )
    run_all(order + copies + locals_)


def scatter(t0, t1, b0, b1):
    paths = lax.axis_size("path")
    groups = lax.axis_size("mod")
    depth, columns = t0.shape
    modules = b0.shape[0]
    rows = depth // paths
    arrived = jax.ShapeDtypeStruct((paths, rows, columns), t0.dtype)
    base = jax.ShapeDtypeStruct((modules, rows, columns), b0.dtype)
    dma = pltpu.SemaphoreType.DMA
    return pl.pallas_call(
        functools.partial(scatter_kernel, paths, groups),
        out_shape=(arrived, arrived, base, base),
        in_specs=[ANY] * 4,
        out_specs=[ANY] * 4,
        scratch_shapes=[dma((2, paths)), dma((2, paths)), dma((2, groups)), dma((2, groups)), dma((4,))],
        compiler_params=pltpu.CompilerParams(has_side_effects=True),
        name="scatter",
    )(t0, t1, b0, b1)


def gather_kernel(paths, v0, v1, r0, r1, send, recv, local):
    p = lax.axis_index("path")
    z = lax.axis_index("mod")
    rows = v0.shape[1]
    copies = []
    locals_ = []
    for level, (v, r) in enumerate(((v0, r0), (v1, r1))):
        mine = r.at[pl.ds(p * rows, rows), :]
        locals_.append(pltpu.make_async_copy(v.at[p], mine, local.at[level]))
        for step in range(paths - 1, 0, -1):
            to = lax.rem(p + step, paths)
            copies.append(
                remote(v.at[to], mine, send.at[level, step], recv.at[level, step], (to, z))
            )
    run_all(copies + locals_)


def gather(v0, v1):
    paths, rows, columns = v0.shape
    result = jax.ShapeDtypeStruct((paths * rows, columns), v0.dtype)
    dma = pltpu.SemaphoreType.DMA
    return pl.pallas_call(
        functools.partial(gather_kernel, paths),
        out_shape=(result, result),
        in_specs=[ANY] * 2,
        out_specs=[ANY] * 2,
        scratch_shapes=[dma((2, paths)), dma((2, paths)), dma((2,))],
        compiler_params=pltpu.CompilerParams(has_side_effects=True),
        name="gather",
    )(v0, v1)


def combine_kernel(level, routing, factor, arrived, base, out, total, fresh):
    paths = arrived.shape[0]
    modules = base.shape[0]
    total[...] = jnp.zeros_like(total)
    for q in range(paths):
        m = routing[q, level]
        total[m] = total[m] + arrived[q].astype(jnp.float32)
    for m in range(modules):
        fresh[m] = (base[m].astype(jnp.float32) + factor[level, m] * total[m]).astype(out.dtype)
    for q in range(paths):
        out[q] = fresh[routing[q, level]]


def combine(level, routing, factor, arrived, base):
    paths, rows, columns = arrived.shape
    modules = base.shape[0]
    block = min(rows, 64)
    smem = pl.BlockSpec(memory_space=pltpu.SMEM)
    return pl.pallas_call(
        functools.partial(combine_kernel, level),
        grid=(rows // block,),
        out_shape=jax.ShapeDtypeStruct(arrived.shape, arrived.dtype),
        in_specs=[
            smem,
            smem,
            pl.BlockSpec((paths, block, columns), lambda i: (0, i, 0)),
            pl.BlockSpec((modules, block, columns), lambda i: (0, i, 0)),
        ],
        out_specs=pl.BlockSpec((paths, block, columns), lambda i: (0, i, 0)),
        scratch_shapes=[
            pltpu.VMEM((modules, block, columns), jnp.float32),
            pltpu.VMEM((modules, block, columns), arrived.dtype),
        ],
        name=f"combine_{level}",
    )(routing, factor, arrived, base)


def body(
    activations,
    cotangent,
    first_weight,
    second_weight,
    first_master,
    second_master,
    first_moment,
    second_moment,
    routing,
):
    inputs_full = lax.all_gather(activations, "mod", axis=1, tiled=True)[0]
    upstream = lax.all_gather(cotangent, "mod", axis=1, tiled=True)[0]

    def base_of(master, moment):
        return (master_factor * master + moment_factor * moment).astype(jnp.bfloat16)

    base_first = base_of(first_master, first_moment)
    base_second = base_of(second_master, second_moment)
    weight_in = first_weight[0]
    weight_out = second_weight[0]
    scale = inputs_full.shape[1] ** (-0.5)
    pre = jnp.dot(inputs_full, weight_in, preferred_element_type=jnp.float32) * scale
    hidden = jax.nn.silu(pre).astype(jnp.bfloat16)
    grad_hidden = jnp.dot(upstream, weight_out, preferred_element_type=jnp.float32) * scale
    grad_out = (
        lax.dot_general(
            upstream, hidden, (((0,), (0,)), ((), ())), preferred_element_type=jnp.float32
        )
        * scale
    )
    trained_out = (weight_out.astype(jnp.float32) - inner_rate * grad_out).astype(jnp.bfloat16)
    sigma = jax.nn.sigmoid(pre)
    grad_pre = (grad_hidden * sigma * (1.0 + pre * (1.0 - sigma))).astype(jnp.bfloat16)
    grad_in = (
        lax.dot_general(
            inputs_full, grad_pre, (((0,), (0,)), ((), ())), preferred_element_type=jnp.float32
        )
        * scale
    )
    trained_in = (weight_in.astype(jnp.float32) - inner_rate * grad_in).astype(jnp.bfloat16)

    arrived_first, arrived_second, own_first, own_second = scatter(
        trained_in, trained_out, base_first, base_second
    )
    modules = first_master.shape[0]
    taken = jnp.sum(
        (jnp.transpose(routing)[:, :, None] == jnp.arange(modules)).astype(jnp.float32), axis=1
    )
    factor = mean_factor / taken
    fresh_first = combine(0, routing, factor, arrived_first, own_first)
    fresh_second = combine(1, routing, factor, arrived_second, own_second)
    first_back, second_back = gather(fresh_first, fresh_second)
    return (first_back[None], second_back[None])


def solution(mesh):
    return jax.shard_map(
        body,
        mesh=mesh,
        in_specs=(
            P("path", "mod", None),
            P("path", "mod", None),
            P("path", None, "mod"),
            P("path", None, "mod"),
            P(None, ("path", "mod"), None),
            P(None, ("path", "mod"), None),
            P(None, ("path", "mod"), None),
            P(None, ("path", "mod"), None),
            P(),
        ),
        out_specs=(P("path", None, "mod"), P("path", None, "mod")),
        check_vma=False,
    )
```

profile of v0, /device:TPU:1, one launch (start us, length us, event | category | flops | bytes accessed | tf_op | source)
XLA Modules:
  0.0 622.2 jit_solution(10252360335064477784)
XLA Ops:
  7.2 0.0 all-gather.5.cloned.1.call-start
  7.2 0.7 all-gather.5.cloned.1.call-update
  7.9 0.0 all-gather.3.cloned.1.call-start
  7.9 0.7 all-gather.3.cloned.1.call-update
  8.6 1.3 copy.17.routing
  10.0 0.8 convert_reduce_fusion
  10.8 0.5 broadcast_divide_fusion.factor
  11.3 17.0 %add_convert_fusion = (bf16[4,128,4096]{2,1,0:T(8,128)(2,1)}, bf16[4,128,4096]{2,1,0:T(8,128)(2,1)}) fusion(f32[4,128,4096]{2,1,0:T(8,128)} %param.16, f32[4,128,4096]{2,1,0:T(8,128)} %param.14, f32[4,128,4096]{2,1,0:T(8,128)} %param.15, f32[4,128,4096]{2,1,0:T(8,128)} %param.13), kind=kLoop, calls=%fused_computation.8 | loop fusion | flops 16777216 | bytes 41943040 | tf_op jit(solution)/shard_map/convert_element_type | solution.py:189
  28.3 64.0 %all-gather.5.cloned.1.call-done = bf16[1,512,4096]{2,1,0:T(8,128)(2,1)} async-done(((bf16[1,128,4096]{2,1,0:T(8,128)(2,1)}), bf16[1,512,4096]{2,1,0:T(8,128)(2,1)}) %all-gather.5.cloned.1.call-update) | async-done | bytes 4194320 | tf_op jit(solution)/shard_map/all_gather | solution.py:185
  92.2 8.1 %fusion.4 = f32[512,1024]{1,0:T(8,128)S(1)} fusion(bf16[1,4096,1024]{2,1,0:T(8,128)(2,1)} %param.11, bf16[1,512,4096]{2,1,0:T(8,128)(2,1)} %all-gather.5.cloned.1.call-done), kind=kOutput, calls=%fused_computation.6 | convolution fusion | flops 4294967296 | bytes 14680064 | tf_op jit(solution)/shard_map/dot_general | solution.py:196
  100.4 72.7 %all-gather.3.cloned.1.call-done = bf16[1,512,4096]{2,1,0:T(8,128)(2,1)} async-done(((bf16[1,128,4096]{2,1,0:T(8,128)(2,1)}), bf16[1,512,4096]{2,1,0:T(8,128)(2,1)}) %all-gather.3.cloned.1.call-update) | async-done | bytes 4194320 | tf_op jit(solution)/shard_map/all_gather | solution.py:186
  173.1 10.7 %multiply_convert_fusion.1 = bf16[512,1024]{1,0:T(8,128)(2,1)} fusion(f32[512,1024]{1,0:T(8,128)S(1)} %fusion.4, bf16[1,4096,1024]{2,1,0:T(8,128)(2,1)} %param.12, bf16[1,512,4096]{2,1,0:T(8,128)(2,1)} %all-gather.3.cloned.1.call-done), kind=kOutput, calls=%fused_computation.15 | convolution fusion | flops 4300734464 | bytes 15728640 | tf_op jit(solution)/shard_map/dot_general | solution.py:198
  183.8 0.0 copy-start
  183.8 11.5 %fusion.t1 = bf16[4096,1024]{1,0:T(8,128)(2,1)} fusion(bf16[1,4096,1024]{2,1,0:T(8,128)(2,1)} %param.12, bf16[1,512,4096]{2,1,0:T(8,128)(2,1)} %all-gather.3.cloned.1.call-done, f32[512,1024]{1,0:T(8,128)S(1)} %fusion.4), kind=kOutput, calls=%fused_computation.1 | convolution fusion | flops 4314890240 | bytes 23068672 | tf_op jit(solution)/shard_map/dot_general | solution.py:200
  195.2 0.0 copy-done
  195.3 9.8 %fusion.1.t0 = bf16[4096,1024]{1,0:T(8,128)(2,1)} fusion(bf16[1,4096,1024]{2,1,0:T(8,128)(2,1)} %param.11, bf16[512,1024]{1,0:T(8,128)(2,1)} %multiply_convert_fusion.1, bf16[1,512,4096]{2,1,0:T(8,128)(2,1)S(1)} %copy-done), kind=kOutput, calls=%fused_computation.3 | convolution fusion | flops 4311744512 | bytes 22020096 | tf_op jit(solution)/shard_map/dot_general | solution.py:209
  205.1 184.4 %scatter.1 = (bf16[8,512,1024]{2,1,0:T(8,128)(2,1)}, bf16[8,512,1024]{2,1,0:T(8,128)(2,1)}, bf16[4,512,1024]{2,1,0:T(8,128)(2,1)}, bf16[4,512,1024]{2,1,0:T(8,128)(2,1)}) custom-call(bf16[4096,1024]{1,0:T(8,128)(2,1)} %fusion.1.t0, bf16[4096,1024]{1,0:T(8,128)(2,1)} %fusion.t1, bf16[4,128,4096]{2,1,0:T(8,128)(2,1)} %get-tuple-element.15.b0, ...), custom_call_target="tpu_custom_call" | custom-call | tf_op jit(solution)/shard_map/scatter/pallas_call | solution.py:94
  389.4 11.3 %combine_1.1.v1 = bf16[8,512,1024]{2,1,0:T(8,128)(2,1)} custom-call(s32[8,2]{1,0:T(8,128)} %copy.17.routing, f32[2,4]{1,0:T(2,128)} %broadcast_divide_fusion.factor, bf16[8,512,1024]{2,1,0:T(8,128)(2,1)} %get-tuple-element.10.arrived, bf16[4,512,1024]{2,1,0:T(8,128)(2,1)} %get-tuple-element.11.base), custom_call_target="tpu_custom_call" | custom-call | tf_op jit(solution)/shard_map/combine_1/pallas_call | solution.py:155
  400.8 11.3 %combine_0.1.v0 = bf16[8,512,1024]{2,1,0:T(8,128)(2,1)} custom-call(s32[8,2]{1,0:T(8,128)} %copy.17.routing, f32[2,4]{1,0:T(2,128)} %broadcast_divide_fusion.factor, bf16[8,512,1024]{2,1,0:T(8,128)(2,1)} %get-tuple-element.8.arrived, bf16[4,512,1024]{2,1,0:T(8,128)(2,1)} %get-tuple-element.9.base), custom_call_target="tpu_custom_call" | custom-call | tf_op jit(solution)/shard_map/combine_0/pallas_call | solution.py:155
  412.1 187.7 %gather.1 = (bf16[4096,1024]{1,0:T(8,128)(2,1)}, bf16[4096,1024]{1,0:T(8,128)(2,1)}) custom-call(bf16[8,512,1024]{2,1,0:T(8,128)(2,1)} %combine_0.1.v0, bf16[8,512,1024]{2,1,0:T(8,128)(2,1)} %combine_1.1.v1), custom_call_target="tpu_custom_call" | custom-call | tf_op jit(solution)/shard_map/gather/pallas_call | solution.py:126
  599.8 7.8 %copy.23 = bf16[1,4096,1024]{2,1,0:T(8,128)(2,1)} copy(bf16[1,4096,1024]{2,1,0:T(8,128)(2,1)} %bitcast.35) | data formatting | bytes 16777216
  607.6 7.8 %copy.24 = bf16[1,4096,1024]{2,1,0:T(8,128)(2,1)} copy(bf16[1,4096,1024]{2,1,0:T(8,128)(2,1)} %bitcast.34) | data formatting | bytes 16777216
Async XLA Ops:
  7.2 85.1 %all-gather.5.cloned.1.call-start = ((), (), s32[]{:S(2)}) async-start(), calls=%async_computation.1 | async-start | bytes 5242880 | tf_op jit(solution)/shard_map/all_gather | solution.py:185
  7.9 165.2 %all-gather.3.cloned.1.call-start = ((), (), s32[]{:S(2)}) async-start(), calls=%async_computation | async-start | bytes 5242880 | tf_op jit(solution)/shard_map/all_gather | solution.py:186
  183.8 11.5 %copy-start = (bf16[1,512,4096]{2,1,0:T(8,128)(2,1)S(1)}, bf16[1,512,4096]{2,1,0:T(8,128)(2,1)}, u32[]{:S(2)}) copy-start(bf16[1,512,4096]{2,1,0:T(8,128)(2,1)} %all-gather.5.cloned.1.call-done) | copy-start | bytes 12582916
Sparse Core Ops, SparseCore 0:
  9.5 82.6 all-gather.4
  93.8 79.2 all-gather.2
where the time goes:
time: 626 us; the launch traced here: 622 us
  Pallas kernels  395 us (63%)
  waiting for transfers between devices  138 us (22%)
  matrix products  40.1 us (6%)
  other arithmetic  18.3 us (3%)
  local copies, waits for them, and re-layouts  16.9 us (3%)
  between operations  14.1 us (2%)
    pallas_call x1, Pallas kernels, gather(): pl.pallas_call(functools.partial(gather_kernel, paths), out_shape=(result...  188 us
    pallas_call x1, Pallas kernels, scatter(): pl.pallas_call(functools.partial(scatter_kernel, paths, groups), out_shap...  184 us
    all_gather x1, waiting for transfers between devices, body(): upstream = lax.all_gather(cotangent, 'mod', axis=1, tiled=True)[0]  72.7 us
    all_gather x1, waiting for transfers between devices, body(): inputs_full = lax.all_gather(activations, 'mod', axis=1, tiled=True)[0]  64 us
    pallas_call x2, Pallas kernels, combine(): pl.pallas_call(functools.partial(combine_kernel, level), grid=(rows // bl...  22.7 us
    convert_element_type x1, other arithmetic, base_of(): (master_factor * master + moment_factor * moment).astype(jnp.bfloat16)  17 us
    unnamed x5, local copies, waits for them, and re-layouts  16.9 us
  transfers between devices with their start and end apart: 2, of which 2 were waited for; matrix products, arithmetic and copies ran while one was open for 4% of the time, Pallas kernels for 0%

commit v1 on v0

v1 whole, which is shorter than its diff:
```python
import functools

import jax
import jax.numpy as jnp
from jax import lax
from jax.experimental import pallas as pl
from jax.experimental.pallas import tpu as pltpu
from jax.sharding import PartitionSpec as P

inner_rate = 1.0
outer_rate = 0.7
momentum_decay = 0.9

mean_factor = outer_rate * (1.0 + momentum_decay)
master_factor = 1.0 - mean_factor
moment_factor = -outer_rate * momentum_decay * momentum_decay

ANY = pl.BlockSpec(memory_space=pl.ANY)
SMEM = pl.BlockSpec(memory_space=pltpu.SMEM)
f32 = jnp.float32
bf16 = jnp.bfloat16


def remote(src, dst, send_sem, recv_sem, where):
    return pltpu.make_async_remote_copy(
        src_ref=src,
        dst_ref=dst,
        send_sem=send_sem,
        recv_sem=recv_sem,
        device_id=where,
        device_id_type=pl.DeviceIdType.MESH,
    )


def aligned(start, size):
    return pl.ds(pl.multiple_of(start, size), size)


def round_kernel(
    paths,
    groups,
    act,
    cot,
    w1,
    w2,
    m1,
    m2,
    u1,
    u2,
    coef,
    routing,
    r1,
    r2,
    b1,
    b2,
    c1,
    c2,
    arr1,
    actv,
    cotv,
    slv,
    w1v,
    w2v,
    arr2,
    hid,
    pre,
    gpre,
    acc,
    fresh,
    chunk,
    base,
    mbuf,
    ubuf,
    obuf,
    zs,
    zr,
    ss,
    sr,
    ws,
    wr,
    hs,
    hr,
    fs,
    fr,
    ts,
    tr,
    bs,
    br,
    os,
    orr,
    loc,
    outloc,
    pipe,
):
    p = lax.axis_index("path")
    z = lax.axis_index("mod")
    tokens, depth = act.shape
    cols = w1.shape[1]
    rows = depth // paths
    sub = m1.shape[1]
    modules = m1.shape[0]
    all_tokens = tokens * groups
    tile = min(cols, 256)
    scale = depth ** (-0.5)
    half = paths // 2
    partner = p + 1 - 2 * lax.rem(p, 2)
    last = groups - 1

    def ahead(step):
        return lax.rem(p + step, paths)

    def behind(step):
        return lax.rem(p + paths - step, paths)

    bufs = (actv, cotv, slv)

    def hop(i, d, s, src, block):
        to = lax.rem(z + 1, groups) if d == 0 else lax.rem(z + last, groups)
        return remote(src, bufs[i].at[block], zs.at[i, d, s], zr.at[i, d, s], (p, to))

    def can_send(d):
        return z < last if d == 0 else z > 0

    def own_send(i, d, src, also=None):
        cond = can_send(d)
        if also is not None:
            cond = jnp.logical_and(cond, also)

        @pl.when(cond)
        def _():
            hop(i, d, 0, src, z).start()

    def block_of(d, s):
        return z - s if d == 0 else z + s

    def present(d, s):
        return z >= s if d == 0 else z + s <= last

    def relay_step(i, s):
        for d in (0, 1):
            block = block_of(d, s)

            @pl.when(present(d, s))
            def _():
                hop(i, d, s - 1, bufs[i].at[block], block).wait_recv()

            @pl.when(jnp.logical_and(present(d, s), can_send(d)))
            def _():
                hop(i, d, s, bufs[i].at[block], block).start()

    def for_blocks(s, work):
        for d in (0, 1):

            @pl.when(present(d, s))
            def _():
                work(block_of(d, s))

    def relay_finish(i):
        for s in range(groups):
            for d in (0, 1):

                @pl.when(jnp.logical_and(present(d, s), can_send(d)))
                def _():
                    block = block_of(d, s)
                    hop(i, d, s, bufs[i].at[block], block).wait_send()

    def next_own(s):
        own_send(1, 0, cot, z == s)
        own_send(1, 1, cot, z == last - s)

    for d in (0, 1):
        own_send(0, d, act)
    next_own(0)

    def slice_copy(step):
        to = ahead(step)
        return remote(
            cot.at[:, aligned(to * rows, rows)], slv.at[z, p], ss.at[step], sr.at[step], (to, z)
        )

    def raw_copy(step):
        to = ahead(step)
        return remote(
            w2.at[aligned(to * rows, rows), :], arr2.at[p], ws.at[step], wr.at[step], (to, z)
        )

    for step in range(1, paths):
        slice_copy(step).start()
    for step in range(1, paths):
        raw_copy(step).start()

    load_act = pltpu.make_async_copy(act, actv.at[z], loc.at[0])
    load_cot = pltpu.make_async_copy(cot, cotv.at[z], loc.at[1])
    load_w1 = pltpu.make_async_copy(w1, w1v, loc.at[2])
    load_w2 = pltpu.make_async_copy(w2, w2v, loc.at[3])
    load_slice = pltpu.make_async_copy(
        cot.at[:, aligned(p * rows, rows)], slv.at[z, p], loc.at[4]
    )
    load_raw = pltpu.make_async_copy(w2.at[aligned(p * rows, rows), :], arr2.at[p], loc.at[5])
    loads = (load_act, load_w1, load_cot, load_w2, load_slice, load_raw)
    for load in loads:
        load.start()

    band = mbuf.shape[1]
    per = sub // band
    for m_ref, u_ref, b_ref in ((m2, u2, b2), (m1, u1, b1)):
        count = modules * per

        def where(i):
            return lax.div(i, per), aligned(lax.rem(i, per) * band, band)

        def fetch(i, slot):
            m, r = where(i)
            return (
                pltpu.make_async_copy(m_ref.at[m, r, :], mbuf.at[slot], pipe.at[0, slot]),
                pltpu.make_async_copy(u_ref.at[m, r, :], ubuf.at[slot], pipe.at[1, slot]),
            )

        def put(i, slot):
            m, r = where(i)
            return pltpu.make_async_copy(obuf.at[slot], b_ref.at[m, r, :], pipe.at[2, slot])

        for c in fetch(0, 0):
            c.start()

        def base_step(i, carry):
            slot = lax.rem(i, 2)
            for c in fetch(i, slot):
                c.wait()

            @pl.when(i + 1 < count)
            def _():
                for c in fetch(i + 1, 1 - slot):
                    c.start()

            @pl.when(i >= 2)
            def _():
                put(i - 2, slot).wait()

            obuf[slot] = (master_factor * mbuf[slot] + moment_factor * ubuf[slot]).astype(bf16)
            put(i, slot).start()
            return carry

        lax.fori_loop(0, count, base_step, 0)
        for i in range(max(0, count - 2), count):
            put(i, i % 2).wait()

    for load in loads:
        load.wait()

    def forward(block):
        here = aligned(block * tokens, tokens)

        def column(n, carry):
            at = aligned(n * tile, tile)
            value = jnp.dot(actv[block], w1v[:, at], preferred_element_type=f32) * scale
            pre[here, at] = value
            hid[p, here, at] = jax.nn.silu(value).astype(bf16)
            return carry

        lax.fori_loop(0, cols // tile, column, 0)

    forward(z)
    for s in range(1, groups):
        relay_step(0, s)
        next_own(s)
        for_blocks(s, forward)

    def hidden_copy(j):
        to = partner if j == 0 else ahead(2 * j)
        return remote(hid.at[p], hid.at[p], hs.at[j], hr.at[j], (to, z))

    def hidden_arrival(j):
        q = partner if j == 0 else behind(2 * j)
        return remote(hid.at[q], hid.at[q], hs.at[j], hr.at[j], (partner, z))

    def hidden_onward(j):
        q = behind(2 * j)
        return remote(hid.at[q], hid.at[q], fs.at[j], fr.at[j], (partner, z))

    def hidden_second(j):
        q = lax.rem(partner + paths - 2 * j, paths)
        return remote(hid.at[q], hid.at[q], fs.at[j], fr.at[j], (partner, z))

    for j in range(half - 1, -1, -1):
        hidden_copy(j).start()

    def backward(block):
        here = aligned(block * tokens, tokens)

        def column(n, carry):
            at = aligned(n * tile, tile)
            value = jnp.dot(cotv[block], w2v[:, at], preferred_element_type=f32) * scale
            before = pre[here, at]
            sigma = jax.nn.sigmoid(before)
            gpre[here, at] = (value * sigma * (1.0 + before * (1.0 - sigma))).astype(bf16)
            return carry

        lax.fori_loop(0, cols // tile, column, 0)

    backward(z)
    for s in range(1, groups):
        relay_step(1, s)
        if s == last:
            for step in range(1, paths):
                q = behind(step)
                remote(
                    slv.at[z, q], slv.at[z, q], ss.at[step], sr.at[step], (ahead(step), z)
                ).wait_recv()
            for d in (0, 1):
                own_send(2, d, slv.at[z])
        for_blocks(s, backward)

    def trained_copy(step):
        to = ahead(step)
        return remote(
            w1v.at[aligned(to * rows, rows), :], arr1.at[p], ts.at[step], tr.at[step], (to, z)
        )

    own_trained = pltpu.make_async_copy(w1v.at[aligned(p * rows, rows), :], arr1.at[p], loc.at[6])

    for step in list(range(1, paths)) + [0]:
        q = ahead(step)
        here = aligned(q * rows, rows)
        lhs = actv[:, :, here].reshape(all_tokens, rows)

        def column(n, carry):
            at = aligned(n * tile, tile)
            grad = lax.dot_general(
                lhs, gpre[:, at], (((0,), (0,)), ((), ())), preferred_element_type=f32
            )
            w1v[here, at] = (w1v[here, at].astype(f32) - inner_rate * (grad * scale)).astype(bf16)
            return carry

        lax.fori_loop(0, cols // tile, column, 0)
        if step == 0:
            own_trained.start()
        else:
            trained_copy(step).start()

    for j in range(1, half):
        hidden_arrival(j).wait_recv()
        hidden_onward(j).start()

    def base_copy(level, step):
        b, c = ((b1, c1), (b2, c2))[level]
        to = lax.rem(z + step, groups)
        return remote(
            b.at[:, :, aligned(to * cols, cols)],
            c.at[:, aligned(z * sub, sub), :],
            bs.at[level, step],
            br.at[level, step],
            (p, to),
        )

    for s in range(1, groups):
        relay_step(2, s)
        if s == max(1, last - 1):
            for level in (1, 0):
                for step in range(1, groups):
                    base_copy(level, step).start()

    hidden_arrival(0).wait_recv()
    for j in range(1, half):
        hidden_second(j).wait_recv()
    for step in range(1, paths):
        q = behind(step)
        remote(
            arr2.at[q], arr2.at[q], ws.at[step], wr.at[step], (ahead(step), z)
        ).wait_recv()

    results = (r1, r2)

    def staged(level, st, q, here):
        if level == 1:
            return arr2.at[q, here, :]
        return w2v.at[aligned((st * paths + q) * sub, sub), :]

    def out_copy(level, st, step):
        j = lax.rem(z + groups - st, groups)
        to = ahead(step)
        src = staged(level, st, to, aligned(j * sub, sub))
        dst = results[level].at[aligned(p * rows + j * sub, sub), :]
        if step == 0:
            return pltpu.make_async_copy(src, dst, outloc.at[level, st])
        return remote(src, dst, os.at[level, st, step], orr.at[level, st, step], (to, z))

    def out_arrival(level, st, step):
        j = lax.rem(z + groups - st, groups)
        q = behind(step)
        dst = results[level].at[aligned(q * rows + j * sub, sub), :]
        return remote(
            dst, dst, os.at[level, st, step], orr.at[level, st, step], (ahead(step), z)
        )

    def combine(level, st, trained):
        j = lax.rem(z + groups - st, groups)
        here = aligned(j * sub, sub)
        b, c = ((b1, c1), (b2, c2))[level]
        acc[...] = jnp.zeros_like(acc)

        def add(q, carry):
            value = trained(q, here)
            for m in range(modules):
                acc[m] = acc[m] + coef[level, m, q] * value
            return carry

        lax.fori_loop(0, paths, add, 0)
        if st == 0:
            src = b.at[:, :, aligned(z * cols, cols)]
        else:
            src = c.at[:, here, :]
            remote(
                src, src, bs.at[level, st], br.at[level, st], (p, lax.rem(z + st, groups))
            ).wait_recv()
        load = pltpu.make_async_copy(src, base, loc.at[7])
        load.start()
        load.wait()
        for m in range(modules):
            fresh[m] = (base[m].astype(f32) + acc[m]).astype(bf16)

        def place(q, carry):
            value = fresh[routing[q, level]]
            if level == 1:
                arr2[q, here, :] = value
            else:
                w2v[aligned((st * paths + q) * sub, sub), :] = value
            return carry

        lax.fori_loop(0, paths, place, 0)
        for step in list(range(1, paths)) + [0]:
            out_copy(level, st, step).start()

    def train_second(q, carry):
        lhs = slv[:, q, :, :].reshape(all_tokens, rows)

        def column(n, carry):
            at = aligned(n * tile, tile)
            grad = lax.dot_general(
                lhs, hid[q, :, at], (((0,), (0,)), ((), ())), preferred_element_type=f32
            )
            raw = arr2[q, :, at].astype(f32)
            arr2[q, :, at] = (raw - inner_rate * (grad * scale)).astype(bf16)
            return carry

        return lax.fori_loop(0, cols // tile, column, carry)

    lax.fori_loop(0, paths, train_second, 0)

    def second(q, here):
        return arr2[q, here, :].astype(f32)

    for st in range(groups):
        combine(1, st, second)

    own_trained.wait()
    for step in range(1, paths):
        q = behind(step)
        remote(
            arr1.at[q], arr1.at[q], ts.at[step], tr.at[step], (ahead(step), z)
        ).wait_recv()

    def first(q, here):
        return chunk[q].astype(f32)

    for st in range(groups):
        j = lax.rem(z + groups - st, groups)
        load = pltpu.make_async_copy(arr1.at[:, aligned(j * sub, sub), :], chunk, loc.at[8])
        load.start()
        load.wait()
        combine(0, st, first)

    for i in range(3):
        relay_finish(i)
    for step in range(1, paths):
        slice_copy(step).wait_send()
        raw_copy(step).wait_send()
        trained_copy(step).wait_send()
    for j in range(half):
        hidden_copy(j).wait_send()
    for j in range(1, half):
        hidden_onward(j).wait_send()
    for level in (1, 0):
        for step in range(1, groups):
            base_copy(level, step).wait_send()
        for st in range(groups):
            out_copy(level, st, 0).wait()
            for step in range(1, paths):
                out_copy(level, st, step).wait_send()
                out_arrival(level, st, step).wait_recv()


def body(
    activations,
    cotangent,
    first_weight,
    second_weight,
    first_master,
    second_master,
    first_moment,
    second_moment,
    routing,
):
    paths = lax.axis_size("path")
    groups = lax.axis_size("mod")
    act = activations[0]
    cot = cotangent[0]
    w1 = first_weight[0]
    w2 = second_weight[0]
    tokens, depth = act.shape
    cols = w1.shape[1]
    rows = depth // paths
    modules, sub, _ = first_master.shape
    band = min(sub, 32)

    onehot = (jnp.transpose(routing)[:, None, :] == jnp.arange(modules)[None, :, None]).astype(f32)
    coef = onehot * (mean_factor / jnp.sum(onehot, axis=2, keepdims=True))

    dma = pltpu.SemaphoreType.DMA
    result = jax.ShapeDtypeStruct((depth, cols), bf16)
    based = jax.ShapeDtypeStruct((modules, sub, depth), bf16)
    moved = jax.ShapeDtypeStruct((modules, rows, cols), bf16)
    outs = pl.pallas_call(
        functools.partial(round_kernel, paths, groups),
        out_shape=(
            result,
            result,
            based,
            based,
            moved,
            moved,
            jax.ShapeDtypeStruct((paths, rows, cols), bf16),
        ),
        in_specs=[ANY] * 8 + [SMEM] * 2,
        out_specs=[ANY] * 7,
        scratch_shapes=[
            pltpu.VMEM((groups, tokens, depth), bf16),
            pltpu.VMEM((groups, tokens, depth), bf16),
            pltpu.VMEM((groups, paths, tokens, rows), bf16),
            pltpu.VMEM((depth, cols), bf16),
            pltpu.VMEM((depth, cols), bf16),
            pltpu.VMEM((paths, rows, cols), bf16),
            pltpu.VMEM((paths, tokens * groups, cols), bf16),
            pltpu.VMEM((tokens * groups, cols), f32),
            pltpu.VMEM((tokens * groups, cols), bf16),
            pltpu.VMEM((modules, sub, cols), f32),
            pltpu.VMEM((modules, sub, cols), bf16),
            pltpu.VMEM((paths, sub, cols), bf16),
            pltpu.VMEM((modules, sub, cols), bf16),
            pltpu.VMEM((2, band, depth), f32),
            pltpu.VMEM((2, band, depth), f32),
            pltpu.VMEM((2, band, depth), bf16),
            dma((3, 2, groups)),
            dma((3, 2, groups)),
            dma((paths,)),
            dma((paths,)),
            dma((paths,)),
            dma((paths,)),
            dma((paths // 2,)),
            dma((paths // 2,)),
            dma((paths // 2,)),
            dma((paths // 2,)),
            dma((paths,)),
            dma((paths,)),
            dma((2, groups)),
            dma((2, groups)),
            dma((2, groups, paths)),
            dma((2, groups, paths)),
            dma((9,)),
            dma((2, groups)),
            dma((3, 2)),
        ],
        compiler_params=pltpu.CompilerParams(
            has_side_effects=True, vmem_limit_bytes=67_000_000
        ),
        name="outer_round",
    )(
        act,
        cot,
        w1,
        w2,
        first_master,
        second_master,
        first_moment,
        second_moment,
        coef,
        routing,
    )
    return (outs[0][None], outs[1][None])


def solution(mesh):
    return jax.shard_map(
        body,
        mesh=mesh,
        in_specs=(
            P("path", "mod", None),
            P("path", "mod", None),
            P("path", None, "mod"),
            P("path", None, "mod"),
            P(None, ("path", "mod"), None),
            P(None, ("path", "mod"), None),
            P(None, ("path", "mod"), None),
            P(None, ("path", "mod"), None),
            P(),
        ),
        out_specs=(P("path", None, "mod"), P("path", None, "mod")),
        check_vma=False,
    )
```

time: 626 us -> 499 us (0.80)
  waiting for transfers between devices: 138 us -> 0 us
  Pallas kernels: 395 us -> 477 us
  matrix products: 40.1 us -> 0 us
  other arithmetic: 18.3 us -> 2.12 us
  between operations: 14.1 us -> 0.64 us
    all_gather x2 -> x0, waiting for transfers between devices: 137 us -> none  [the longest x1 72.7 us: body(): upstream = lax.all_gather(cotangent, 'mod', axis=1, tiled=True)[0]]
    pallas_call x4 -> x1, Pallas kernels: 395 us -> 477 us  [body(): pl.pallas_call(functools.partial(round_kernel, paths, groups), out_shape=...]
    dot_general x4 -> x0, matrix products: 40.1 us -> none  [the longest x1 11.5 us: body(): lax.dot_general(upstream, hidden, (((0,), (0,)), ((), ())), preferred_ele...]
    convert_element_type x1 -> x0, other arithmetic: 17 us -> none  [base_of(): (master_factor * master + moment_factor * moment).astype(jnp.bfloat16)]
    unnamed x5 -> x3, local copies, waits for them, and re-layouts: 16.9 us -> 16.9 us
  transfers between devices with their start and end apart: 2 -> 0, of which waited for: 2 -> 0; matrix products, arithmetic and copies ran while one was open for 4% -> 0% of each run, Pallas kernels for 0% -> 0%
where the time goes in v1:
time: 499 us; the launch traced here: 497 us
  Pallas kernels  477 us (96%)
  local copies, waits for them, and re-layouts  16.9 us (3%)
    pallas_call x1, Pallas kernels, body(): pl.pallas_call(functools.partial(round_kernel, paths, groups), out_shape=...  477 us
    unnamed x3, local copies, waits for them, and re-layouts  16.9 us

profile of v1, /device:TPU:1, one launch (start us, length us, event | category | flops | bytes accessed | tf_op | source)
XLA Modules:
  0.0 497.1 jit_solution(11317580936289822457)
XLA Ops:
  0.6 0.8 convert_reduce_fusion
  1.4 1.3 fusion.coef
  2.8 1.3 copy.11.routing
  4.1 477.5 %outer_round.1 = (bf16[4096,1024]{1,0:T(8,128)(2,1)}, bf16[4096,1024]{1,0:T(8,128)(2,1)}, bf16[4,128,4096]{2,1,0:T(8,128)(2,1)}, bf16[4,128,4096]{2,1,0:T(8,128)...) custom-call(bf16[128,4096]{1,0:T(8,128)(2,1)} %bitcast.11, ...), custom_call_target="tpu_custom_call" | custom-call | tf_op jit(solution)/shard_map/outer_round/pallas_call | solution.py:523
  481.6 7.8 %copy.14 = bf16[1,4096,1024]{2,1,0:T(8,128)(2,1)} copy(bf16[1,4096,1024]{2,1,0:T(8,128)(2,1)} %bitcast.8) | data formatting | bytes 16777216
  489.4 7.8 %copy.15 = bf16[1,4096,1024]{2,1,0:T(8,128)(2,1)} copy(bf16[1,4096,1024]{2,1,0:T(8,128)(2,1)} %bitcast.7) | data formatting | bytes 16777216
  (1 shorter events, 0.0 us)

commit v2 on v1

--- a/solution.py
+++ b/solution.py
@@ -17,6 +17,7 @@
 
 ANY = pl.BlockSpec(memory_space=pl.ANY)
 SMEM = pl.BlockSpec(memory_space=pltpu.SMEM)
+MESH = pl.DeviceIdType.MESH
 f32 = jnp.float32
 bf16 = jnp.bfloat16
 
@@ -47,7 +48,6 @@
     m2,
     u1,
     u2,
-    coef,
     routing,
     r1,
     r2,
@@ -91,6 +91,7 @@
     loc,
     outloc,
     pipe,
+    done,
 ):
     p = lax.axis_index("path")
     z = lax.axis_index("mod")
@@ -121,12 +122,8 @@
     def can_send(d):
         return z < last if d == 0 else z > 0
 
-    def own_send(i, d, src, also=None):
-        cond = can_send(d)
-        if also is not None:
-            cond = jnp.logical_and(cond, also)
-
-        @pl.when(cond)
+    def own_send(i, d, src):
+        @pl.when(can_send(d))
         def _():
             hop(i, d, 0, src, z).start()
 
@@ -164,13 +161,18 @@
                     block = block_of(d, s)
                     hop(i, d, s, bufs[i].at[block], block).wait_send()
 
-    def next_own(s):
-        own_send(1, 0, cot, z == s)
-        own_send(1, 1, cot, z == last - s)
-
-    for d in (0, 1):
-        own_send(0, d, act)
-    next_own(0)
+    barrier = pltpu.get_barrier_semaphore()
+    for step in range(1, paths):
+        pl.semaphore_signal(barrier, inc=1, device_id=(ahead(step), z), device_id_type=MESH)
+    for step in range(1, groups):
+        pl.semaphore_signal(
+            barrier, inc=1, device_id=(p, lax.rem(z + step, groups)), device_id_type=MESH
+        )
+    pl.semaphore_wait(barrier, paths + groups - 2)
+
+    for i, own in enumerate((act, cot)):
+        for d in (0, 1):
+            own_send(i, d, own)
 
     def slice_copy(step):
         to = ahead(step)
@@ -203,10 +205,14 @@
 
     band = mbuf.shape[1]
     per = sub // band
-    for m_ref, u_ref, b_ref in ((m2, u2, b2), (m1, u1, b1)):
-        count = modules * per
+    count = modules * per // 2
+
+    def base_part(part):
+        level, first_band = (1, 1, 0, 0)[part], (part % 2) * count
+        m_ref, u_ref, b_ref = ((m1, u1, b1), (m2, u2, b2))[level]
 
         def where(i):
+            i = first_band + i
             return lax.div(i, per), aligned(lax.rem(i, per) * band, band)
 
         def fetch(i, slot):
@@ -220,18 +226,18 @@
             m, r = where(i)
             return pltpu.make_async_copy(obuf.at[slot], b_ref.at[m, r, :], pipe.at[2, slot])
 
-        for c in fetch(0, 0):
-            c.start()
+        for copy in fetch(0, 0):
+            copy.start()
 
         def base_step(i, carry):
             slot = lax.rem(i, 2)
-            for c in fetch(i, slot):
-                c.wait()
+            for copy in fetch(i, slot):
+                copy.wait()
 
             @pl.when(i + 1 < count)
             def _():
-                for c in fetch(i + 1, 1 - slot):
-                    c.start()
+                for copy in fetch(i + 1, 1 - slot):
+                    copy.start()
 
             @pl.when(i >= 2)
             def _():
@@ -241,9 +247,10 @@
             put(i, slot).start()
             return carry
 
-        lax.fori_loop(0, count, base_step, 0)
-        for i in range(max(0, count - 2), count):
-            put(i, i % 2).wait()
+        with jax.named_scope("base"):
+            lax.fori_loop(0, count, base_step, 0)
+            for i in range(max(0, count - 2), count):
+                put(i, i % 2).wait()
 
     for load in loads:
         load.wait()
@@ -261,9 +268,11 @@
         lax.fori_loop(0, cols // tile, column, 0)
 
     forward(z)
+    parts = list(range(4))
     for s in range(1, groups):
+        if parts:
+            base_part(parts.pop(0))
         relay_step(0, s)
-        next_own(s)
         for_blocks(s, forward)
 
     def hidden_copy(j):
@@ -300,6 +309,8 @@
 
     backward(z)
     for s in range(1, groups):
+        if parts:
+            base_part(parts.pop(0))
         relay_step(1, s)
         if s == last:
             for step in range(1, paths):
@@ -338,10 +349,6 @@
         else:
             trained_copy(step).start()
 
-    for j in range(1, half):
-        hidden_arrival(j).wait_recv()
-        hidden_onward(j).start()
-
     def base_copy(level, step):
         b, c = ((b1, c1), (b2, c2))[level]
         to = lax.rem(z + step, groups)
@@ -353,12 +360,34 @@
             (p, to),
         )
 
+    while parts:
+        base_part(parts.pop(0))
     for s in range(1, groups):
         relay_step(2, s)
-        if s == max(1, last - 1):
-            for level in (1, 0):
-                for step in range(1, groups):
-                    base_copy(level, step).start()
+        if s == 1:
+            for j in range(1, half):
+                hidden_arrival(j).wait_recv()
+                hidden_onward(j).start()
+
+    def inner(at):
+        return jnp.logical_and(at > 0, at < last)
+
+    def base_sends(early):
+        for step in range(1, groups):
+            within = jnp.logical_and(inner(z), inner(lax.rem(z + step, groups)))
+
+            @pl.when(within if early else jnp.logical_not(within))
+            def _():
+                base_copy(1, step).start()
+
+    base_sends(True)
+    for step in range(1, groups):
+        pl.semaphore_signal(
+            done, inc=1, device_id=(p, lax.rem(z + step, groups)), device_id_type=MESH
+        )
+    with jax.named_scope("column"):
+        pl.semaphore_wait(done, groups - 1)
+    base_sends(False)
 
     hidden_arrival(0).wait_recv()
     for j in range(1, half):
@@ -393,6 +422,17 @@
             dst, dst, os.at[level, st, step], orr.at[level, st, step], (ahead(step), z)
         )
 
+    def factor(level, m):
+        taken = jnp.int32(0)
+        for q in range(paths):
+            taken = taken + jnp.where(routing[q, level] == m, 1, 0)
+        value = jnp.float32(mean_factor)
+        for k in range(2, paths + 1):
+            value = jnp.where(taken == k, jnp.float32(mean_factor / k), value)
+        return value
+
+    factors = [[factor(level, m) for m in range(modules)] for level in range(2)]
+
     def combine(level, st, trained):
         j = lax.rem(z + groups - st, groups)
         here = aligned(j * sub, sub)
@@ -402,7 +442,8 @@
         def add(q, carry):
             value = trained(q, here)
             for m in range(modules):
-                acc[m] = acc[m] + coef[level, m, q] * value
+                weight = jnp.where(routing[q, level] == m, factors[level][m], 0.0)
+                acc[m] = acc[m] + weight * value
             return carry
 
         lax.fori_loop(0, paths, add, 0)
@@ -452,6 +493,8 @@
 
     for st in range(groups):
         combine(1, st, second)
+    for step in range(1, groups):
+        base_copy(0, step).start()
 
     own_trained.wait()
     for step in range(1, paths):
@@ -488,6 +531,44 @@
             for step in range(1, paths):
                 out_copy(level, st, step).wait_send()
                 out_arrival(level, st, step).wait_recv()
+
+
+def deliver_kernel(block, a0, a1, o0, o1, buf, sem):
+    copies = []
+    for level, (a, o) in enumerate(((a0, o0), (a1, o1))):
+        for i in range(a.shape[0] // block):
+            here = pl.ds(i * block, block)
+            slot = buf.at[level, here, :]
+            copies.append(
+                (
+                    pltpu.make_async_copy(a.at[here, :], slot, sem.at[level, i, 0]),
+                    pltpu.make_async_copy(slot, o.at[here, :], sem.at[level, i, 1]),
+                )
+            )
+    for fetch, _ in copies:
+        fetch.start()
+    for fetch, put in copies:
+        fetch.wait()
+        put.start()
+    for _, put in copies:
+        put.wait()
+
+
+def deliver(a0, a1):
+    depth, cols = a0.shape
+    block = depth // 8
+    return pl.pallas_call(
+        functools.partial(deliver_kernel, block),
+        out_shape=(jax.ShapeDtypeStruct(a0.shape, a0.dtype),) * 2,
+        in_specs=[ANY] * 2,
+        out_specs=[ANY] * 2,
+        scratch_shapes=[
+            pltpu.VMEM((2, depth, cols), a0.dtype),
+            pltpu.SemaphoreType.DMA((2, depth // block, 2)),
+        ],
+        compiler_params=pltpu.CompilerParams(vmem_limit_bytes=67_000_000),
+        name="deliver",
+    )(a0, a1)
 
 
 def body(
@@ -513,9 +594,6 @@
     modules, sub, _ = first_master.shape
     band = min(sub, 32)
 
-    onehot = (jnp.transpose(routing)[:, None, :] == jnp.arange(modules)[None, :, None]).astype(f32)
-    coef = onehot * (mean_factor / jnp.sum(onehot, axis=2, keepdims=True))
-
     dma = pltpu.SemaphoreType.DMA
     result = jax.ShapeDtypeStruct((depth, cols), bf16)
     based = jax.ShapeDtypeStruct((modules, sub, depth), bf16)
@@ -531,7 +609,7 @@
             moved,
             jax.ShapeDtypeStruct((paths, rows, cols), bf16),
         ),
-        in_specs=[ANY] * 8 + [SMEM] * 2,
+        in_specs=[ANY] * 8 + [SMEM],
         out_specs=[ANY] * 7,
         scratch_shapes=[
             pltpu.VMEM((groups, tokens, depth), bf16),
@@ -569,9 +647,10 @@
             dma((9,)),
             dma((2, groups)),
             dma((3, 2)),
+            pltpu.SemaphoreType.REGULAR,
         ],
         compiler_params=pltpu.CompilerParams(
-            has_side_effects=True, vmem_limit_bytes=67_000_000
+            has_side_effects=True, vmem_limit_bytes=67_000_000, collective_id=0
         ),
         name="outer_round",
     )(
@@ -583,10 +662,10 @@
         second_master,
         first_moment,
         second_moment,
-        coef,
         routing,
     )
-    return (outs[0][None], outs[1][None])
+    first_back, second_back = deliver(outs[0], outs[1])
+    return (first_back[None], second_back[None])
 
 
 def solution(mesh):

time: 499 us -> 442 us (0.89)
  Pallas kernels: 477 us -> 439 us
  local copies, waits for them, and re-layouts: 16.9 us -> 1.35 us
    pallas_call x1, Pallas kernels: 477 us -> 427 us  [body(): pl.pallas_call(functools.partial(round_kernel, paths, groups), out_shape=...]
    unnamed x3 -> x1, local copies, waits for them, and re-layouts: 16.9 us -> 1.35 us
    pallas_call x0 -> x1, Pallas kernels: none -> 12 us  [deliver(): pl.pallas_call(functools.partial(deliver_kernel, block), out_shape=(jax.S...]
where the time goes in v2:
time: 442 us; the launch traced here: 441 us
  Pallas kernels  439 us (99%)
    pallas_call x1, Pallas kernels, body(): pl.pallas_call(functools.partial(round_kernel, paths, groups), out_shape=...  427 us
    pallas_call x1, Pallas kernels, deliver(): pl.pallas_call(functools.partial(deliver_kernel, block), out_shape=(jax.S...  12 us

profile of v2, /device:TPU:1, one launch (start us, length us, event | category | flops | bytes accessed | tf_op | source)
XLA Modules:
  0.0 440.9 jit_solution(8354037580340624522)
XLA Ops:
  0.6 1.3 copy.11.routing
  2.0 426.7 %outer_round.1 = (bf16[4096,1024]{1,0:T(8,128)(2,1)}, bf16[4096,1024]{1,0:T(8,128)(2,1)}, bf16[4,128,4096]{2,1,0:T(8,128)(2,1)}, bf16[4,128,4096]{2,1,0:T(8,128)...) custom-call(bf16[128,4096]{1,0:T(8,128)(2,1)} %bitcast.8, ...), custom_call_target="tpu_custom_call" | custom-call | tf_op jit(solution)/shard_map/outer_round/pallas_call | solution.py:601
  428.7 12.0 %deliver.1 = (bf16[4096,1024]{1,0:T(8,128)(2,1)}, bf16[4096,1024]{1,0:T(8,128)(2,1)}) custom-call(bf16[4096,1024]{1,0:T(8,128)(2,1)} %get-tuple-element.6.a0, bf16[4096,1024]{1,0:T(8,128)(2,1)} %get-tuple-element.7.a1), custom_call_target="tpu_custom_call" | custom-call | tf_op jit(solution)/shard_map/deliver/pallas_call | solution.py:560

commit v3 on v2

--- a/solution.py
+++ b/solution.py
@@ -91,7 +91,10 @@
     loc,
     outloc,
     pipe,
-    done,
+    ps,
+    pr,
+    relayed,
+    based,
 ):
     p = lax.axis_index("path")
     z = lax.axis_index("mod")
@@ -270,28 +273,57 @@
     forward(z)
     parts = list(range(4))
     for s in range(1, groups):
-        if parts:
-            base_part(parts.pop(0))
+        for _ in range(2 if s == 2 else 1):
+            if parts:
+                base_part(parts.pop(0))
         relay_step(0, s)
         for_blocks(s, forward)
 
+    spread = half == 4
+
+    def flip(at, bit):
+        return at + bit - 2 * bit * lax.rem(lax.div(at, bit), 2)
+
+    def source(at, j):
+        if j == 0:
+            return flip(at, 1)
+        if spread:
+            return flip(at, 2) if j == 1 else flip(at, 4) if j == 2 else flip(flip(at, 2), 4)
+        return lax.rem(at + paths - 2 * j, paths)
+
+    direct = 3 if spread else half
+
     def hidden_copy(j):
-        to = partner if j == 0 else ahead(2 * j)
+        to = source(p, j) if j == 0 or spread else ahead(2 * j)
         return remote(hid.at[p], hid.at[p], hs.at[j], hr.at[j], (to, z))
 
     def hidden_arrival(j):
-        q = partner if j == 0 else behind(2 * j)
+        q = source(p, j)
         return remote(hid.at[q], hid.at[q], hs.at[j], hr.at[j], (partner, z))
 
+    def hidden_half(k):
+        piece = hid.at[source(p, 1 + k), pl.ds(k * (all_tokens // 2), all_tokens // 2), :]
+        return remote(piece, piece, ps.at[k], pr.at[k], (source(p, 2 - k), z))
+
+    def half_arrival(k):
+        piece = hid.at[source(p, 3), pl.ds(k * (all_tokens // 2), all_tokens // 2), :]
+        return remote(piece, piece, ps.at[k], pr.at[k], (partner, z))
+
+    def pass_halves():
+        for k in range(2):
+            with jax.named_scope("halfwait"):
+                hidden_arrival(1 + k).wait_recv()
+            hidden_half(k).start()
+
     def hidden_onward(j):
-        q = behind(2 * j)
+        q = source(p, j)
         return remote(hid.at[q], hid.at[q], fs.at[j], fr.at[j], (partner, z))
 
     def hidden_second(j):
-        q = lax.rem(partner + paths - 2 * j, paths)
+        q = source(partner, j)
         return remote(hid.at[q], hid.at[q], fs.at[j], fr.at[j], (partner, z))
 
-    for j in range(half - 1, -1, -1):
+    for j in range(direct - 1, -1, -1):
         hidden_copy(j).start()
 
     def backward(block):
@@ -307,10 +339,36 @@
 
         lax.fori_loop(0, cols // tile, column, 0)
 
+    def base_copy(level, step):
+        b, c = ((b1, c1), (b2, c2))[level]
+        to = lax.rem(z + step, groups)
+        return remote(
+            b.at[:, :, aligned(to * cols, cols)],
+            c.at[:, aligned(z * sub, sub), :],
+            bs.at[level, step],
+            br.at[level, step],
+            (p, to),
+        )
+
+    def inner(at):
+        return jnp.logical_and(at > 0, at < last)
+
+    def base_sends(level, early):
+        for step in range(1, groups):
+            within = jnp.logical_and(inner(z), inner(lax.rem(z + step, groups)))
+
+            @pl.when(within if early else jnp.logical_not(within))
+            def _():
+                base_copy(level, step).start()
+
     backward(z)
     for s in range(1, groups):
-        if parts:
-            base_part(parts.pop(0))
+        if s == last:
+            while parts:
+                base_part(parts.pop(0))
+            base_sends(1, True)
+            if spread:
+                pass_halves()
         relay_step(1, s)
         if s == last:
             for step in range(1, paths):
@@ -349,45 +407,27 @@
         else:
             trained_copy(step).start()
 
-    def base_copy(level, step):
-        b, c = ((b1, c1), (b2, c2))[level]
-        to = lax.rem(z + step, groups)
-        return remote(
-            b.at[:, :, aligned(to * cols, cols)],
-            c.at[:, aligned(z * sub, sub), :],
-            bs.at[level, step],
-            br.at[level, step],
-            (p, to),
-        )
-
-    while parts:
-        base_part(parts.pop(0))
     for s in range(1, groups):
         relay_step(2, s)
-        if s == 1:
-            for j in range(1, half):
-                hidden_arrival(j).wait_recv()
-                hidden_onward(j).start()
-
-    def inner(at):
-        return jnp.logical_and(at > 0, at < last)
-
-    def base_sends(early):
+
+    def tell_column(sem):
         for step in range(1, groups):
-            within = jnp.logical_and(inner(z), inner(lax.rem(z + step, groups)))
-
-            @pl.when(within if early else jnp.logical_not(within))
-            def _():
-                base_copy(1, step).start()
-
-    base_sends(True)
-    for step in range(1, groups):
-        pl.semaphore_signal(
-            done, inc=1, device_id=(p, lax.rem(z + step, groups)), device_id_type=MESH
-        )
+            pl.semaphore_signal(
+                sem, inc=1, device_id=(p, lax.rem(z + step, groups)), device_id_type=MESH
+            )
+
+    base_sends(0, True)
+    tell_column(relayed)
+    for j in range(1, half):
+        if not spread:
+            hidden_arrival(j).wait_recv()
+        if spread and j == 3:
+            for k in range(2):
+                half_arrival(k).wait_recv()
+        hidden_onward(j).start()
     with jax.named_scope("column"):
-        pl.semaphore_wait(done, groups - 1)
-    base_sends(False)
+        pl.semaphore_wait(relayed, groups - 1)
+    base_sends(1, False)
 
     hidden_arrival(0).wait_recv()
     for j in range(1, half):
@@ -493,8 +533,10 @@
 
     for st in range(groups):
         combine(1, st, second)
-    for step in range(1, groups):
-        base_copy(0, step).start()
+    tell_column(based)
+    with jax.named_scope("column2"):
+        pl.semaphore_wait(based, groups - 1)
+    base_sends(0, False)
 
     own_trained.wait()
     for step in range(1, paths):
@@ -519,8 +561,11 @@
         slice_copy(step).wait_send()
         raw_copy(step).wait_send()
         trained_copy(step).wait_send()
-    for j in range(half):
+    for j in range(direct):
         hidden_copy(j).wait_send()
+    if spread:
+        for k in range(2):
+            hidden_half(k).wait_send()
     for j in range(1, half):
         hidden_onward(j).wait_send()
     for level in (1, 0):
@@ -647,6 +692,9 @@
             dma((9,)),
             dma((2, groups)),
             dma((3, 2)),
+            dma((2,)),
+            dma((2,)),
+            pltpu.SemaphoreType.REGULAR,
             pltpu.SemaphoreType.REGULAR,
         ],
         compiler_params=pltpu.CompilerParams(

time: 442 us -> 437 us (0.989)
  Pallas kernels: 439 us -> 432 us
    pallas_call x1, Pallas kernels: 427 us -> 420 us  [body(): pl.pallas_call(functools.partial(round_kernel, paths, groups), out_shape=...]
where the time goes in v3:
time: 437 us; the launch traced here: 434 us
  Pallas kernels  432 us (99%)
    pallas_call x1, Pallas kernels, body(): pl.pallas_call(functools.partial(round_kernel, paths, groups), out_shape=...  420 us
    pallas_call x1, Pallas kernels, deliver(): pl.pallas_call(functools.partial(deliver_kernel, block), out_shape=(jax.S...  12 us

profile of v3, /device:TPU:1, one launch (start us, length us, event | category | flops | bytes accessed | tf_op | source)
XLA Modules:
  0.0 434.3 jit_solution(10160315400322507675)
XLA Ops:
  0.6 1.3 copy.11.routing
  2.0 420.2 %outer_round.1 = (bf16[4096,1024]{1,0:T(8,128)(2,1)}, bf16[4096,1024]{1,0:T(8,128)(2,1)}, bf16[4,128,4096]{2,1,0:T(8,128)(2,1)}, bf16[4,128,4096]{2,1,0:T(8,128)...) custom-call(bf16[128,4096]{1,0:T(8,128)(2,1)} %bitcast.8, ...), custom_call_target="tpu_custom_call" | custom-call | tf_op jit(solution)/shard_map/outer_round/pallas_call | solution.py:646
  422.2 12.0 %deliver.1 = (bf16[4096,1024]{1,0:T(8,128)(2,1)}, bf16[4096,1024]{1,0:T(8,128)(2,1)}) custom-call(bf16[4096,1024]{1,0:T(8,128)(2,1)} %get-tuple-element.6.a0, bf16[4096,1024]{1,0:T(8,128)(2,1)} %get-tuple-element.7.a1), custom_call_target="tpu_custom_call" | custom-call | tf_op jit(solution)/shard_map/deliver/pallas_call | solution.py:605
